TPU v7x, 32 devices: a whole 2x2x4 slice. The times are simulated.
32 devices in a mesh: dp: 4 (over z), row: 2 (over y), col: 4 (over x, core).
Axes of the slice: x: 2, y: 2, z: 4, core: 2. Of those that a mesh axis runs over, the one named last changes fastest.
Arguments:
- activations: bfloat16 [4096, 4096], P('dp', 'col'), may hold values from -6 to 6
- out_grad: bfloat16 [4096, 14336], P('dp', 'row'), may hold values from -6 to 6
- weight: float32 [2, 7168, 4096], P('row', 'dp', 'col'), as said below
- step_size: float32 [2, 7168], P('row'), may hold values from 0.001 to 0.016
Outputs:
- input_grad: bfloat16 [4096, 4096], P(('dp', 'row'), 'col')
- weight_grad: float32 [2, 7168, 4096], P('row', 'dp', 'col')
- step_grad: float32 [2, 7168], P('row', 'dp')
Inputs may be any that keep to these rules, and one draw needn't show every extreme that they name: Each latent weight divided by its row's step lies at least 0.1 away from every multiple of one half.
All inputs are finite; a program needn't handle non-finite values.
Results may differ from a plain program's by a relative error of at most 0.0096.
Values may be sent and summed in bfloat16 or wider, within the bound.
A program may use at most 128 MiB of HBM per device.

v0:
```python
import jax
import jax.numpy as jnp
from jax import lax
from jax.sharding import PartitionSpec as P

D = 4096


def quantize(latent, scales):
    ratio = latent / scales[:, None]
    clipped = jnp.clip(ratio, -8.0, 7.0)
    levels = jnp.floor(clipped + 0.5)
    inside = jnp.where((ratio >= -8.0) & (ratio <= 7.0), 1.0, 0.0).astype(jnp.float32)
    factor = jnp.where(inside > 0.5, levels - ratio, clipped)
    quantized = (levels * scales[:, None]).astype(jnp.bfloat16)
    return (quantized, inside, factor)


def shards(activations, out_grad, weight, step_size):
    own_count = weight.shape[1]
    position = lax.axis_index("dp")
    scales = step_size[0]
    own_scales = lax.dynamic_slice_in_dim(scales, position * own_count, own_count, 0)
    grad_factor = 1.0 / (7.0 * D) ** 0.5
    products = lax.dot_general(
        out_grad, activations, (((0,), (0,)), ((), ())), preferred_element_type=jnp.float32
    )
    own_quantized, own_inside, own_factor = quantize(weight[0], own_scales)
    quantized = lax.all_gather(own_quantized, "dp", axis=0, tiled=True)
    summed = lax.psum_scatter(products, "dp", scatter_dimension=0, tiled=True)
    step_rows = lax.psum(jnp.sum(summed * own_factor, axis=1) * grad_factor, "col")
    weight_grad = (summed * own_inside)[None]
    input_grad = lax.psum_scatter(
        jnp.dot(out_grad, quantized, preferred_element_type=jnp.float32),
        "row",
        scatter_dimension=0,
        tiled=True,
    ).astype(jnp.bfloat16)
    return (input_grad, weight_grad, step_rows[None])


def solution(mesh):
    in_specs = (P("dp", "col"), P("dp", "row"), P("row", "dp", "col"), P("row", None))
    out_specs = (P(("dp", "row"), "col"), P("row", "dp", "col"), P("row", "dp"))
    return jax.shard_map(shards, mesh=mesh, in_specs=in_specs, out_specs=out_specs, check_vma=False)
```

profile of v0, /device:TPU:0, one launch (start us, length us, event | category | flops | bytes accessed | tf_op | source)
XLA Modules:
  0.0 865.8 jit_solution(2981315032197045996)
XLA Ops:
  7.2 0.0 copy-start
  7.2 0.0 reduce-scatter.5.cloned.1.call-start
  7.2 1.5 copy-done
  8.8 24.0 %fusion.1 = f32[7168,1024]{1,0:T(8,128)} fusion(bf16[1024,7168]{1,0:T(8,128)(2,1)} %param.5, bf16[1024,1024]{1,0:T(8,128)(2,1)S(1)} %copy-done), kind=kOutput, calls=%fused_computation.11 | convolution fusion | flops 15032385536 | bytes 46137344 | tf_op jit(solution)/shard_map/dot_general | solution.py:25
  32.7 0.0 reduce-scatter.5.cloned.1.call-update
  32.8 0.0 all-gather.2.cloned.1.call-start
  32.8 0.7 dynamic-slice_reduce_fusion
  33.5 483.8 %reduce-scatter.5.cloned.1.call-done = f32[1792,1024]{1,0:T(8,128)} async-done(((f32[7168,1024]{1,0:T(8,128)}), f32[1792,1024]{1,0:T(8,128)}) %reduce-scatter.5.cloned.1.call-update) | async-done | bytes 7340048 | tf_op jit(solution)/shard_map/reduce_scatter | solution.py:30
  517.3 10.0 %multiply_reduce_fusion = (f32[1792]{0:T(1024)S(1)}, f32[1,1792,1024]{2,1,0:T(8,128)}, bf16[1792,1024]{1,0:T(8,128)(2,1)}) fusion(f32[1792,1024]{1,0:T(8,128)} %reduce-scatter.5.cloned.1.call-done, f32[1792]{0:T(1024)S(1)} %dynamic-slice_reduce_fusion, f32[1,1792,1024]{2,1,0:T(8,128)} %param.6), kind=kLoop, calls=%fused_computation.4 | loop fusion | flops 29358336 | bytes 25704448 | tf_op jit(solution)/shard_map/reduce_sum | solution.py:31
  527.3 0.0 all-gather.2.cloned.1.call-update
  527.3 0.2 reduce-scatter.3.cloned.1.call-start
  527.6 254.5 %all-gather.2.cloned.1.call-done = bf16[7168,1024]{1,0:T(8,128)(2,1)} async-done(((bf16[1792,1024]{1,0:T(8,128)(2,1)}), bf16[7168,1024]{1,0:T(8,128)(2,1)}) %all-gather.2.cloned.1.call-update) | async-done | bytes 14680080 | tf_op jit(solution)/shard_map/all_gather | solution.py:29
  782.0 0.0 copy-start.1
  782.0 21.4 %convolution_bitcast_fusion = f32[1024,1024]{0,1:T(8,128)} fusion(bf16[7168,1024]{1,0:T(8,128)(2,1)} %all-gather.2.cloned.1.call-done, bf16[1024,7168]{1,0:T(8,128)(2,1)} %param.5), kind=kOutput, calls=%fused_computation.8 | convolution fusion | flops 15032385536 | bytes 33554432 | tf_op jit(solution)/shard_map/dot_general | solution.py:34
  803.5 0.0 reduce-scatter.3.cloned.1.call-update
  803.5 7.5 psum.7
  811.0 45.2 %reduce-scatter.3.cloned.1.call-done = f32[512,1024]{0,1:T(8,128)} async-done(((f32[1024,1024]{0,1:T(8,128)}), f32[512,1024]{0,1:T(8,128)}) %reduce-scatter.3.cloned.1.call-update) | async-done | bytes 2097168 | tf_op jit(solution)/shard_map/reduce_scatter | solution.py:33
  856.2 1.7 convert_element_type.7
  857.9 1.3 copy.7
  859.3 0.0 copy-done.1
  (2 shorter events, 0.0 us)
Async XLA Ops:
  7.2 1.6 copy-start
  7.2 510.1 %reduce-scatter.5.cloned.1.call-start = ((), (), s32[]{:S(2)}) async-start(), calls=%async_computation.4 | async-start | bytes 36700160 | tf_op jit(solution)/shard_map/reduce_scatter | solution.py:30
  32.8 749.3 %all-gather.2.cloned.1.call-start = ((), (), s32[]{:S(2)}) async-start(), calls=%async_computation.2 | async-start | bytes 18350080 | tf_op jit(solution)/shard_map/all_gather | solution.py:29
  527.3 328.9 %reduce-scatter.3.cloned.1.call-start = ((), (), s32[]{:S(2)}) async-start(), calls=%async_computation.3 | async-start | bytes 6291456 | tf_op jit(solution)/shard_map/reduce_scatter | solution.py:33
  782.0 77.2 %copy-start.1 = (bf16[1024,1024]{1,0:T(8,128)(2,1)S(1)}, bf16[1024,1024]{1,0:T(8,128)(2,1)}, u32[]{:S(2)}) copy-start(bf16[1024,1024]{1,0:T(8,128)(2,1)} %param.4) | copy-start | bytes 6291460
Sparse Core Ops, SparseCore 0:
  32.9 484.3 reduce-scatter.4
  527.5 254.5 all-gather.1
  803.6 52.5 reduce-scatter.2
where the time goes:
time: 866 us
  waiting for transfers between devices  783 us (90%)
  matrix products  45.4 us (5%)
  between operations  13.8 us (2%)
  other arithmetic  11.7 us (1%)
    reduce_scatter x1, waiting for transfers between devices, shards(): summed = lax.psum_scatter(products, 'dp', scatter_dimension=0, tiled=True)  484 us
    all_gather x1, waiting for transfers between devices, shards(): quantized = lax.all_gather(own_quantized, 'dp', axis=0, tiled=True)  254 us
    reduce_scatter x1, waiting for transfers between devices, shards(): lax.psum_scatter(jnp.dot(out_grad, quantized, preferred_element_type=jnp....  45.2 us
    dot_general x1, matrix products, shards(): lax.dot_general(out_grad, activations, (((0,), (0,)), ((), ())), preferre...  24 us
    dot_general x1, matrix products, shards(): jnp.dot(out_grad, quantized, preferred_element_type=jnp.float32)  21.4 us
  transfers between devices with their start and end apart: 3, of which 3 were waited for; matrix products, arithmetic and copies ran while one was open for 0% of the time, Pallas kernels for 0%

commit v1 on v0

v1 whole, which is shorter than its diff:
```python
import jax
import jax.numpy as jnp
from jax import lax
from jax.sharding import PartitionSpec as P

D = 4096


def quantize(latent, scales):
    ratio = latent / scales[:, None]
    clipped = jnp.clip(ratio, -8.0, 7.0)
    levels = jnp.floor(clipped + 0.5)
    inside = jnp.where((ratio >= -8.0) & (ratio <= 7.0), 1.0, 0.0).astype(jnp.float32)
    factor = jnp.where(inside > 0.5, levels - ratio, clipped)
    quantized = (levels * scales[:, None]).astype(jnp.bfloat16)
    return (quantized, inside, factor)


def shift(block, axis, count, by):
    return lax.ppermute(block, axis, [(i, (i + by) % count) for i in range(count)])


def swap(block, axis, count, bit):
    return lax.ppermute(block, axis, [(i, i ^ bit) for i in range(count)])


def gather_rows(block, axis, count):
    position = lax.axis_index(axis)
    bit = 1
    bits = []
    while bit < count:
        bits.append(bit)
        bit *= 2
    pieces = {0: block}
    for bit in reversed(bits):
        held = dict(pieces)
        for key in held:
            pieces[key ^ bit] = swap(held[key], axis, count, bit)
    parts = [pieces[key] for key in range(count)]
    for bit in bits:
        flag = (position & bit) != 0
        parts = [
            jnp.where(flag, parts[key ^ bit], parts[key]) for key in range(count)
        ]
    return jnp.concatenate(parts, axis=0)


def make_shards(n_dp, n_row, n_col):
    def shards(activations, out_grad, weight, step_size):
        own_count = weight.shape[1]
        tokens = out_grad.shape[0]
        dp = lax.axis_index("dp")
        row = lax.axis_index("row")
        col = lax.axis_index("col")
        scales = step_size[0]
        own_scales = lax.dynamic_slice_in_dim(scales, dp * own_count, own_count, 0)
        grad_factor = 1.0 / (7.0 * D) ** 0.5

        share = tokens // n_col
        half = tokens // n_row
        mine = lax.dynamic_slice_in_dim(out_grad, col * share, share, 0)
        ring = lax.dynamic_slice_in_dim(activations, row * half, half, 0)
        grads, acts = [], []
        for k in range(1, n_dp):
            target = (dp + k) % n_dp
            chunk = lax.dynamic_slice_in_dim(mine, target * own_count, own_count, 1)
            grads.append(shift(chunk, "dp", n_dp, k))
            ring = shift(ring, "dp", n_dp, 1)
            acts.append(ring)

        quantized, inside, factor = quantize(weight[0], own_scales)
        own_grad = lax.dynamic_slice_in_dim(out_grad, dp * own_count, own_count, 1)

        def reduced(grad):
            size = tokens
            bit = n_row // 2
            if bit == 0:
                return jnp.dot(grad, quantized, preferred_element_type=jnp.float32)
            size //= 2
            upper = ((row // bit) % 2).astype(jnp.int32)
            sent = lax.dynamic_slice_in_dim(grad, (1 - upper) * size, size, 0)
            kept = lax.dynamic_slice_in_dim(grad, upper * size, size, 0)
            out = jnp.dot(sent, quantized, preferred_element_type=jnp.float32).astype(jnp.bfloat16)
            came = swap(out, "row", n_row, bit)
            total = jnp.dot(kept, quantized, preferred_element_type=jnp.float32) + came.astype(jnp.float32)
            bit //= 2
            while bit:
                size //= 2
                upper = (row // bit) % 2 == 1
                low, high = total[:size], total[size:]
                came = swap(jnp.where(upper, low, high).astype(jnp.bfloat16), "row", n_row, bit)
                total = jnp.where(upper, high, low) + came.astype(jnp.float32)
                bit //= 2
            return total

        products = lax.dot_general(
            own_grad, activations, (((0,), (0,)), ((), ())), preferred_element_type=jnp.float32
        )
        own_total = reduced(own_grad)
        running = None
        for k in range(1, n_dp):
            grad = gather_rows(grads[k - 1], "col", n_col)
            total = reduced(grad)
            if running is not None:
                total = total + running.astype(jnp.float32)
            running = shift(total.astype(jnp.bfloat16), "dp", n_dp, 1)
            act = gather_rows(acts[k - 1], "row", n_row)
            products = products + lax.dot_general(
                grad, act, (((0,), (0,)), ((), ())), preferred_element_type=jnp.float32
            )
        if running is not None:
            own_total = own_total + running.astype(jnp.float32)
        input_grad = own_total.astype(jnp.bfloat16)
        step_rows = lax.psum(jnp.sum(products * factor, axis=1) * grad_factor, "col")
        weight_grad = (products * inside)[None]
        return (input_grad, weight_grad, step_rows[None])

    return shards


def solution(mesh):
    in_specs = (P("dp", "col"), P("dp", "row"), P("row", "dp", "col"), P("row", None))
    out_specs = (P(("dp", "row"), "col"), P("row", "dp", "col"), P("row", "dp"))
    shards = make_shards(mesh.shape["dp"], mesh.shape["row"], mesh.shape["col"])
    return jax.shard_map(shards, mesh=mesh, in_specs=in_specs, out_specs=out_specs, check_vma=False)
```

time: 866 us -> 331 us (0.38)
  waiting for transfers between devices: 783 us -> 179 us
  starting transfers between devices: 0.3 us -> 27.4 us
  local copies, waits for them, and re-layouts: 3.59 us -> 24.9 us
  matrix products: 45.4 us -> 64 us
  other arithmetic: 11.7 us -> 27.8 us
  between operations: 13.8 us -> 0.93 us
    reduce_scatter x2 -> x0, waiting for transfers between devices: 529 us -> none  [the longest x1 484 us: shards(): summed = lax.psum_scatter(products, 'dp', scatter_dimension=0, tiled=True)]
    all_gather x1 -> x0, waiting for transfers between devices: 254 us -> none  [shards(): quantized = lax.all_gather(own_quantized, 'dp', axis=0, tiled=True)]
    ppermute x0 -> x25, waiting for transfers between devices: none -> 179 us  [the longest x9 115 us: shift(): lax.ppermute(block, axis, [(i, (i + by) % count) for i in range(count)])]
    ppermute x0 -> x25, starting transfers between devices: none -> 27.4 us  [the longest x9 15 us: shift(): lax.ppermute(block, axis, [(i, (i + by) % count) for i in range(count)])]
    dot_general x2 -> x12, matrix products: 45.4 us -> 64 us  [the longest x3 27.1 us: shards(): lax.dot_general(grad, act, (((0,), (0,)), ((), ())), preferred_element_ty...]
    unnamed x5 -> x42, local copies, waits for them, and re-layouts: 2.86 us -> 18.4 us
    select_n x0 -> x6, other arithmetic: none -> 9.59 us  [gather_rows(): jnp.where(flag, parts[key ^ bit], parts[key])]
  transfers between devices with their start and end apart: 3 -> 25, of which waited for: 3 -> 14; matrix products, arithmetic and copies ran while one was open for 0% -> 26% of each run, Pallas kernels for 0% -> 0%
where the time goes in v1:
time: 331 us
  waiting for transfers between devices  179 us (54%)
  matrix products  64 us (19%)
  other arithmetic  27.8 us (8%)
  starting transfers between devices  27.4 us (8%)
  local copies, waits for them, and re-layouts  24.9 us (8%)
  blocking collectives  6.73 us (2%)
    ppermute x9, waiting for transfers between devices, shift(): lax.ppermute(block, axis, [(i, (i + by) % count) for i in range(count)])  115 us
    ppermute x16, waiting for transfers between devices, swap(): return lax.ppermute(block, axis, [(i, i ^ bit) for i in range(count)])  63.8 us
    dot_general x3, matrix products, shards(): lax.dot_general(grad, act, (((0,), (0,)), ((), ())), preferred_element_ty...  27.1 us
    unnamed x42, local copies, waits for them, and re-layouts  18.4 us
    ppermute x9, starting transfers between devices, shift(): lax.ppermute(block, axis, [(i, (i + by) % count) for i in range(count)])  15 us
    dot_general x4, matrix products, reduced(): jnp.dot(kept, quantized, preferred_element_type=jnp.float32)  14.5 us
    dot_general x4, matrix products, reduced(): jnp.dot(sent, quantized, preferred_element_type=jnp.float32)  14.2 us
    ppermute x16, starting transfers between devices, swap(): return lax.ppermute(block, axis, [(i, i ^ bit) for i in range(count)])  12.3 us
  transfers between devices with their start and end apart: 25, of which 14 were waited for; matrix products, arithmetic and copies ran while one was open for 26% of the time, Pallas kernels for 0%

profile of v1, /device:TPU:0, one launch (start us, length us, event | category | flops | bytes accessed | tf_op | source)
XLA Modules:
  0.0 330.7 jit_solution(6011322174611351139)
XLA Ops:
  12.6 20.0 %collective-permute-done.19 = bf16[512,1024]{1,0:T(8,128)(2,1)S(1)} collective-permute-done((bf16[512,1024]{1,0:T(8,128)(2,1)}, bf16[512,1024]{1,0:T(8,128)(2,1)S(1)}, u32[]{:S(2)}, u32[]{:S(2)}) %collective-permute-start.19) | collective-permute-done | bytes 1048608 | tf_op jit(solution)/shard_map/ppermute | solution.py:20
  36.1 16.3 %collective-permute-done.11 = bf16[256,1792]{1,0:T(8,128)(2,1)} collective-permute-done((bf16[256,1792]{1,0:T(8,128)(2,1)S(1)}, bf16[256,1792]{1,0:T(8,128)(2,1)}, u32[]{:S(2)}, u32[]{:S(2)}) %collective-permute-start.11) | collective-permute-done | bytes 917536 | tf_op jit(solution)/shard_map/ppermute | solution.py:20
  54.1 8.4 %copy.7 = f32[1,1792,1024]{1,2,0:T(8,128)} copy(f32[1,1792,1024]{2,1,0:T(8,128)} %param.6) | data formatting | bytes 14680064 | tf_op args[2]
  63.3 7.9 %collective-permute-done.1 = bf16[256,1792]{1,0:T(8,128)(2,1)} collective-permute-done((bf16[256,1792]{1,0:T(8,128)(2,1)}, bf16[256,1792]{1,0:T(8,128)(2,1)}, u32[]{:S(2)}, u32[]{:S(2)}) %collective-permute-start.1) | collective-permute-done | bytes 917536 | tf_op jit(solution)/shard_map/ppermute | solution.py:20
  72.7 37.7 %collective-permute-done.6 = bf16[256,1792]{1,0:T(8,128)(2,1)} collective-permute-done((bf16[256,1792]{1,0:T(8,128)(2,1)}, bf16[256,1792]{1,0:T(8,128)(2,1)}, u32[]{:S(2)}, u32[]{:S(2)}) %collective-permute-start.6) | collective-permute-done | bytes 917536 | tf_op jit(solution)/shard_map/ppermute | solution.py:20
  112.0 8.2 %fusion.1 = f32[1792,1024]{0,1:T(8,128)} fusion(bf16[1024,1024]{1,0:T(8,128)(2,1)S(1)} %copy-done, bf16[1024,7168]{1,0:T(8,128)(2,1)} %param.5, s32[]{:T(128)S(6)} %select_n.216), kind=kOutput, calls=%fused_computation.12 | convolution fusion | flops 3758096384 | bytes 13107204 | tf_op jit(solution)/shard_map/dot_general | solution.py:96
  122.3 10.7 %collective-permute-done.7 = bf16[256,1792]{1,0:T(8,128)(2,1)S(1)} collective-permute-done((bf16[256,1792]{1,0:T(8,128)(2,1)}, bf16[256,1792]{1,0:T(8,128)(2,1)S(1)}, u32[]{:S(2)}, u32[]{:S(2)}) %collective-permute-start.7) | collective-permute-done | bytes 917536 | tf_op jit(solution)/shard_map/ppermute | solution.py:24
  132.9 5.6 %collective-permute-done.21 = bf16[512,1024]{1,0:T(8,128)(2,1)S(1)} collective-permute-done((bf16[512,1024]{1,0:T(8,128)(2,1)S(1)}, bf16[512,1024]{1,0:T(8,128)(2,1)S(1)}, u32[]{:S(2)}, u32[]{:S(2)}) %collective-permute-start.21) | collective-permute-done | bytes 1048608 | tf_op jit(solution)/shard_map/ppermute | solution.py:20
  141.9 6.7 %fusion.3 = f32[1792,1024]{0,1:T(8,128)} fusion(bf16[512,1024]{1,0:T(8,128)(2,1)S(1)} %get-tuple-element.27, bf16[512,1024]{1,0:T(8,128)(2,1)S(1)} %get-tuple-element.26, bf16[256,1792]{1,0:T(8,128)(2,1)S(1)} %get-tuple-element.23, bf16[256,1792]{1,0:T(8,128)(2,1)S(1)} %get-tuple-element.22, bf16[256,1792]{1,0:T(8,128)(2,1)S(1)} %get-tuple-element.21, ...), kind=kOutput, calls=%fused_computation.14 | convolution fusion | flops 3776970752 | bytes 13107200 | tf_op jit(solution)/shard_map/dot_general | solution.py:108
  148.6 6.0 %collective-permute-start.23 = (bf16[512,1024]{1,0:T(8,128)(2,1)S(1)}, bf16[512,1024]{1,0:T(8,128)(2,1)S(1)}, u32[]{:S(2)}, u32[]{:S(2)}) collective-permute-start(bf16[512,1024]{1,0:T(8,128)(2,1)S(1)} %collective-permute-done.21), channel_id=1, source_target_pairs={{0,8},{8,16},{16,24},{24,0},{1,9},{9,17},{17,25},{25,1},{2,10},{10... | collective-permute-start | bytes 3145736 | tf_op jit(solution)/shard_map/ppermute | solution.py:20
  159.4 17.6 %collective-permute-done.23 = bf16[512,1024]{1,0:T(8,128)(2,1)S(1)} collective-permute-done((bf16[512,1024]{1,0:T(8,128)(2,1)S(1)}, bf16[512,1024]{1,0:T(8,128)(2,1)S(1)}, u32[]{:S(2)}, u32[]{:S(2)}) %collective-permute-start.23) | collective-permute-done | bytes 1048608 | tf_op jit(solution)/shard_map/ppermute | solution.py:20
  179.7 6.7 %fusion.7 = f32[1792,1024]{0,1:T(8,128)} fusion(bf16[512,1024]{1,0:T(8,128)(2,1)S(1)} %get-tuple-element.29, bf16[512,1024]{1,0:T(8,128)(2,1)S(1)} %get-tuple-element.28, bf16[256,1792]{1,0:T(8,128)(2,1)S(1)} %get-tuple-element.19, bf16[256,1792]{1,0:T(8,128)(2,1)S(1)} %get-tuple-element.18, bf16[256,1792]{1,0:T(8,128)(2,1)S(1)} %get-tuple-element.17, ...), kind=kOutput, calls=%fused_computation.18 | convolution fusion | flops 3776970752 | bytes 13107200 | tf_op jit(solution)/shard_map/dot_general | solution.py:108
  186.4 14.6 %collective-permute-done.24 = bf16[512,1024]{1,0:T(8,128)(2,1)S(1)} collective-permute-done((bf16[512,1024]{1,0:T(8,128)(2,1)S(1)}, bf16[512,1024]{1,0:T(8,128)(2,1)S(1)}, u32[]{:S(2)}, u32[]{:S(2)}) %collective-permute-start.24) | collective-permute-done | bytes 1048608 | tf_op jit(solution)/shard_map/ppermute | solution.py:24
  202.4 13.7 %add_add_fusion = f32[1792,1024]{0,1:T(8,128)} fusion(f32[1792,1024]{0,1:T(8,128)} %fusion.7, f32[1792,1024]{0,1:T(8,128)} %fusion.1, f32[1792,1024]{0,1:T(8,128)} %fusion.3, bf16[512,1024]{1,0:T(8,128)(2,1)} %get-tuple-element.25, bf16[512,1024]{1,0:T(8,128)(2,1)} %get-tuple-element.24, bf16[256,1792]{1,0:T(8,128)(2,1)} %get-tuple-element.15, ...), kind=kOutput, calls=%fused_computation.5 | convolution fusion | flops 3782475776 | bytes 35127296 | tf_op jit(solution)/shard_map/dot_general | solution.py:108
  216.2 8.0 %multiply_reduce_fusion = (f32[1792]{0:T(1024)S(1)}, f32[1,1792,1024]{1,2,0:T(8,128)}, bf16[1792,1024]{0,1:T(8,128)(2,1)S(1)}) fusion(f32[1792,1024]{0,1:T(8,128)} %add_add_fusion, f32[1792]{0:T(1024)S(1)} %dynamic-slice_reduce_fusion, f32[1,1792,1024]{1,2,0:T(8,128)S(1)} %bitcast.20), kind=kLoop, calls=%fused_computation.4 | loop fusion | flops 29358336 | bytes 25704448 | tf_op jit(solution)/shard_map/reduce_sum | solution.py:114
  227.7 5.1 %pad_maximum_fusion.1 = bf16[1024,1792]{1,0:T(8,128)(2,1)S(1)} fusion(bf16[256,1792]{1,0:T(8,128)(2,1)} %copy-done.14, bf16[256,1792]{1,0:T(8,128)(2,1)} %copy-done.13, bf16[256,1792]{1,0:T(8,128)(2,1)S(1)} %copy-done.12, bf16[256,1792]{1,0:T(8,128)(2,1)S(1)} %copy-done.10), kind=kLoop, calls=%fused_computation.10 | loop fusion | flops 14680064 | bytes 7340032 | tf_op jit(solution)/shard_map/concatenate | solution.py:45
  236.6 17.0 %collective-permute-done.15 = bf16[512,1024]{1,0:T(8,128)(2,1)} collective-permute-done((bf16[512,1024]{1,0:T(8,128)(2,1)}, bf16[512,1024]{1,0:T(8,128)(2,1)}, u32[]{:S(2)}, u32[]{:S(2)}) %collective-permute-start.15) | collective-permute-done | bytes 1048608 | tf_op jit(solution)/shard_map/ppermute | solution.py:24
  263.6 12.4 %collective-permute-done.10 = bf16[512,1024]{1,0:T(8,128)(2,1)S(1)} collective-permute-done((bf16[512,1024]{1,0:T(8,128)(2,1)S(1)}, bf16[512,1024]{1,0:T(8,128)(2,1)S(1)}, u32[]{:S(2)}, u32[]{:S(2)}) %collective-permute-start.10) | collective-permute-done | bytes 1048608 | tf_op jit(solution)/shard_map/ppermute | solution.py:24
  282.8 5.9 %fusion.30 = bf16[512,1024]{1,0:T(8,128)(2,1)} fusion(bf16[1792,1024]{0,1:T(8,128)(2,1)} %copy-done.15, bf16[1024,7168]{1,0:T(8,128)(2,1)} %param.5, s32[]{:T(128)S(6)} %select_n.219, s32[]{:T(128)S(6)} %select_n.217), kind=kOutput, calls=%fused_computation.45 | convolution fusion | flops 1879572480 | bytes 6553608 | tf_op jit(solution)/shard_map/dot_general | solution.py:83
  289.2 9.2 %collective-permute-done.5 = bf16[512,1024]{1,0:T(8,128)(2,1)S(1)} collective-permute-done((bf16[512,1024]{1,0:T(8,128)(2,1)}, bf16[512,1024]{1,0:T(8,128)(2,1)S(1)}, u32[]{:S(2)}, u32[]{:S(2)}) %collective-permute-start.5) | collective-permute-done | bytes 1048608 | tf_op jit(solution)/shard_map/ppermute | solution.py:24
  298.4 5.7 %collective-permute-done.17 = bf16[512,1024]{1,0:T(8,128)(2,1)S(1)} collective-permute-done((bf16[512,1024]{1,0:T(8,128)(2,1)}, bf16[512,1024]{1,0:T(8,128)(2,1)S(1)}, u32[]{:S(2)}, u32[]{:S(2)}) %collective-permute-start.17) | collective-permute-done | bytes 1048608 | tf_op jit(solution)/shard_map/ppermute | solution.py:20
  307.3 8.4 %copy.8 = f32[1,1792,1024]{2,1,0:T(8,128)} copy(f32[1,1792,1024]{1,2,0:T(8,128)} %get-tuple-element.7) | data formatting | bytes 14680064
  315.7 6.7 %psum.7 = f32[1,1792]{1,0:T(1,128)} all-reduce(f32[1,1792]{1,0:T(1,128)S(1)} %broadcast_in_dim.19), channel_id=1, replica_groups=mesh['dp'=4,'row'=2,'col'=4] {'col'}, use_global_device_ids=true, to_apply=%region_1.2 | all-reduce | flops 1792 | bytes 14336 | tf_op jit(solution)/shard_map/psum | solution.py:114
  322.4 4.9 %fusion.28 = f32[512,1024]{1,0:T(8,128)S(1)} fusion(bf16[1792,1024]{0,1:T(8,128)(2,1)} %copy-done.15, bf16[1024,7168]{1,0:T(8,128)(2,1)} %param.5, s32[]{:T(128)S(6)} %select_n.215, s32[]{:T(128)S(6)} %select_n.217), kind=kOutput, calls=%fused_computation.43 | convolution fusion | flops 1879048192 | bytes 7602184 | tf_op jit(solution)/shard_map/dot_general | solution.py:85
  (98 shorter events, 66.5 us)
Async XLA Ops:
  3.3 29.3 %collective-permute-start.19 = (bf16[512,1024]{1,0:T(8,128)(2,1)}, bf16[512,1024]{1,0:T(8,128)(2,1)S(1)}, u32[]{:S(2)}, u32[]{:S(2)}) collective-permute-start(bf16[512,1024]{1,0:T(8,128)(2,1)} %constant_dynamic-slice_fusion), channel_id=1, source_target_pairs={{0,8},{8,16},{16,24},{24,0},{1,9},{9,17},{17,25},{25,1},{2,10},{10... | collective-permute-start | bytes 3145736 | tf_op jit(solution)/shard_map/ppermute | solution.py:20
  11.0 41.4 %collective-permute-start.11 = (bf16[256,1792]{1,0:T(8,128)(2,1)S(1)}, bf16[256,1792]{1,0:T(8,128)(2,1)}, u32[]{:S(2)}, u32[]{:S(2)}) collective-permute-start(bf16[256,1792]{1,0:T(8,128)(2,1)S(1)} %get-tuple-element.10), channel_id=1, source_target_pairs={{0,8},{8,16},{16,24},{24,0},{1,9},{9,17},{17,25},{25,1},{2,10},{10... | collective-permute-start | bytes 2752520 | tf_op jit(solution)/shard_map/ppermute | solution.py:20
  32.6 79.4 %collective-permute-start.20 = (bf16[512,1024]{1,0:T(8,128)(2,1)S(1)}, bf16[512,1024]{1,0:T(8,128)(2,1)}, u32[]{:S(2)}, u32[]{:S(2)}) collective-permute-start(bf16[512,1024]{1,0:T(8,128)(2,1)S(1)} %collective-permute-done.19), channel_id=1, source_target_pairs={{0,4},{4,0},{1,5},{5,1},{2,6},{6,2},{3,7},{7,3},{8,12},{12,8},{9,1... | collective-permute-start | bytes 3145736 | tf_op jit(solution)/shard_map/ppermute | solution.py:24
  34.3 36.9 %collective-permute-start.1 = (bf16[256,1792]{1,0:T(8,128)(2,1)}, bf16[256,1792]{1,0:T(8,128)(2,1)}, u32[]{:S(2)}, u32[]{:S(2)}) collective-permute-start(bf16[256,1792]{1,0:T(8,128)(2,1)} %get-tuple-element.8), channel_id=1, source_target_pairs={{0,24},{8,0},{16,8},{24,16},{1,25},{9,1},{17,9},{25,17},{2,26},{10... | collective-permute-start | bytes 2752520 | tf_op jit(solution)/shard_map/ppermute | solution.py:20
  36.1 74.4 %collective-permute-start.6 = (bf16[256,1792]{1,0:T(8,128)(2,1)}, bf16[256,1792]{1,0:T(8,128)(2,1)}, u32[]{:S(2)}, u32[]{:S(2)}) collective-permute-start(bf16[256,1792]{1,0:T(8,128)(2,1)} %get-tuple-element.9), channel_id=1, source_target_pairs={{0,16},{8,24},{16,0},{24,8},{1,17},{9,25},{17,1},{25,9},{2,18},{10... | collective-permute-start | bytes 2752520 | tf_op jit(solution)/shard_map/ppermute | solution.py:20
  52.4 59.6 %collective-permute-start.12 = (bf16[256,1792]{1,0:T(8,128)(2,1)}, bf16[256,1792]{1,0:T(8,128)(2,1)}, u32[]{:S(2)}, u32[]{:S(2)}) collective-permute-start(bf16[256,1792]{1,0:T(8,128)(2,1)} %collective-permute-done.11), channel_id=1, source_target_pairs={{0,2},{1,3},{2,0},{3,1},{4,6},{5,7},{6,4},{7,5},{8,10},{9,11},{10,... | collective-permute-start | bytes 2752520 | tf_op jit(solution)/shard_map/ppermute | solution.py:24
  63.3 58.9 %collective-permute-start.14 = (bf16[256,1792]{1,0:T(8,128)(2,1)}, bf16[256,1792]{1,0:T(8,128)(2,1)S(1)}, u32[]{:S(2)}, u32[]{:S(2)}) collective-permute-start(bf16[256,1792]{1,0:T(8,128)(2,1)} %collective-permute-done.11), channel_id=1, source_target_pairs={{0,1},{1,0},{2,3},{3,2},{4,5},{5,4},{6,7},{7,6},{8,9},{9,8},{10,11... | collective-permute-start | bytes 2752520 | tf_op jit(solution)/shard_map/ppermute | solution.py:24
  71.2 50.4 %collective-permute-start.2 = (bf16[256,1792]{1,0:T(8,128)(2,1)}, bf16[256,1792]{1,0:T(8,128)(2,1)S(1)}, u32[]{:S(2)}, u32[]{:S(2)}) collective-permute-start(bf16[256,1792]{1,0:T(8,128)(2,1)} %collective-permute-done.1), channel_id=1, source_target_pairs={{0,2},{1,3},{2,0},{3,1},{4,6},{5,7},{6,4},{7,5},{8,10},{9,11},{10,... | collective-permute-start | bytes 2752520 | tf_op jit(solution)/shard_map/ppermute | solution.py:24
  110.5 22.4 %collective-permute-start.7 = (bf16[256,1792]{1,0:T(8,128)(2,1)}, bf16[256,1792]{1,0:T(8,128)(2,1)S(1)}, u32[]{:S(2)}, u32[]{:S(2)}) collective-permute-start(bf16[256,1792]{1,0:T(8,128)(2,1)} %collective-permute-done.6), channel_id=1, source_target_pairs={{0,2},{1,3},{2,0},{3,1},{4,6},{5,7},{6,4},{7,5},{8,10},{9,11},{10,... | collective-permute-start | bytes 2752520 | tf_op jit(solution)/shard_map/ppermute | solution.py:24
  112.0 26.6 %collective-permute-start.21 = (bf16[512,1024]{1,0:T(8,128)(2,1)S(1)}, bf16[512,1024]{1,0:T(8,128)(2,1)S(1)}, u32[]{:S(2)}, u32[]{:S(2)}) collective-permute-start(bf16[512,1024]{1,0:T(8,128)(2,1)S(1)} %collective-permute-done.19), channel_id=1, source_target_pairs={{0,8},{8,16},{16,24},{24,0},{1,9},{9,17},{17,25},{25,1},{2,10},{10... | collective-permute-start | bytes 3145736 | tf_op jit(solution)/shard_map/ppermute | solution.py:20
  112.0 26.6 %collective-permute-start.13 = (bf16[256,1792]{1,0:T(8,128)(2,1)}, bf16[256,1792]{1,0:T(8,128)(2,1)S(1)}, u32[]{:S(2)}, u32[]{:S(2)}) collective-permute-start(bf16[256,1792]{1,0:T(8,128)(2,1)} %collective-permute-done.12), channel_id=1, source_target_pairs={{0,1},{1,0},{2,3},{3,2},{4,5},{5,4},{6,7},{7,6},{8,9},{9,8},{10,11... | collective-permute-start | bytes 2752520 | tf_op jit(solution)/shard_map/ppermute | solution.py:24
  121.6 27.0 %collective-permute-start.4 = (bf16[256,1792]{1,0:T(8,128)(2,1)}, bf16[256,1792]{1,0:T(8,128)(2,1)S(1)}, u32[]{:S(2)}, u32[]{:S(2)}) collective-permute-start(bf16[256,1792]{1,0:T(8,128)(2,1)} %collective-permute-done.1), channel_id=1, source_target_pairs={{0,1},{1,0},{2,3},{3,2},{4,5},{5,4},{6,7},{7,6},{8,9},{9,8},{10,11... | collective-permute-start | bytes 2752520 | tf_op jit(solution)/shard_map/ppermute | solution.py:24
  122.2 35.7 %collective-permute-start.9 = (bf16[256,1792]{1,0:T(8,128)(2,1)}, bf16[256,1792]{1,0:T(8,128)(2,1)S(1)}, u32[]{:S(2)}, u32[]{:S(2)}) collective-permute-start(bf16[256,1792]{1,0:T(8,128)(2,1)} %collective-permute-done.6), channel_id=1, source_target_pairs={{0,1},{1,0},{2,3},{3,2},{4,5},{5,4},{6,7},{7,6},{8,9},{9,8},{10,11... | collective-permute-start | bytes 2752520 | tf_op jit(solution)/shard_map/ppermute | solution.py:24
  132.9 21.7 %collective-permute-start.3 = (bf16[256,1792]{1,0:T(8,128)(2,1)S(1)}, bf16[256,1792]{1,0:T(8,128)(2,1)S(1)}, u32[]{:S(2)}, u32[]{:S(2)}) collective-permute-start(bf16[256,1792]{1,0:T(8,128)(2,1)S(1)} %collective-permute-done.2), channel_id=1, source_target_pairs={{0,1},{1,0},{2,3},{3,2},{4,5},{5,4},{6,7},{7,6},{8,9},{9,8},{10,11... | collective-permute-start | bytes 2752520 | tf_op jit(solution)/shard_map/ppermute | solution.py:24
  138.5 41.0 %collective-permute-start.22 = (bf16[512,1024]{1,0:T(8,128)(2,1)S(1)}, bf16[512,1024]{1,0:T(8,128)(2,1)S(1)}, u32[]{:S(2)}, u32[]{:S(2)}) collective-permute-start(bf16[512,1024]{1,0:T(8,128)(2,1)S(1)} %collective-permute-done.21), channel_id=1, source_target_pairs={{0,4},{4,0},{1,5},{5,1},{2,6},{6,2},{3,7},{7,3},{8,12},{12,8},{9,1... | collective-permute-start | bytes 3145736 | tf_op jit(solution)/shard_map/ppermute | solution.py:24
  148.6 28.3 %collective-permute-start.23 = (bf16[512,1024]{1,0:T(8,128)(2,1)S(1)}, bf16[512,1024]{1,0:T(8,128)(2,1)S(1)}, u32[]{:S(2)}, u32[]{:S(2)}) collective-permute-start(bf16[512,1024]{1,0:T(8,128)(2,1)S(1)} %collective-permute-done.21), channel_id=1, source_target_pairs={{0,8},{8,16},{16,24},{24,0},{1,9},{9,17},{17,25},{25,1},{2,10},{10... | collective-permute-start | bytes 3145736 | tf_op jit(solution)/shard_map/ppermute | solution.py:20
  177.0 24.0 %collective-permute-start.24 = (bf16[512,1024]{1,0:T(8,128)(2,1)S(1)}, bf16[512,1024]{1,0:T(8,128)(2,1)S(1)}, u32[]{:S(2)}, u32[]{:S(2)}) collective-permute-start(bf16[512,1024]{1,0:T(8,128)(2,1)S(1)} %collective-permute-done.23), channel_id=1, source_target_pairs={{0,4},{4,0},{1,5},{5,1},{2,6},{6,2},{3,7},{7,3},{8,12},{12,8},{9,1... | collective-permute-start | bytes 3145736 | tf_op jit(solution)/shard_map/ppermute | solution.py:24
  227.2 26.4 %collective-permute-start.15 = (bf16[512,1024]{1,0:T(8,128)(2,1)}, bf16[512,1024]{1,0:T(8,128)(2,1)}, u32[]{:S(2)}, u32[]{:S(2)}) collective-permute-start(bf16[512,1024]{1,0:T(8,128)(2,1)} %fusion.39), channel_id=1, source_target_pairs={{0,4},{4,0},{1,5},{5,1},{2,6},{6,2},{3,7},{7,3},{8,12},{12,8},{9,1... | collective-permute-start | bytes 3145736 | tf_op jit(solution)/shard_map/ppermute | solution.py:24
  235.0 40.9 %collective-permute-start.10 = (bf16[512,1024]{1,0:T(8,128)(2,1)S(1)}, bf16[512,1024]{1,0:T(8,128)(2,1)S(1)}, u32[]{:S(2)}, u32[]{:S(2)}) collective-permute-start(bf16[512,1024]{1,0:T(8,128)(2,1)S(1)} %fusion.36), channel_id=1, source_target_pairs={{0,4},{4,0},{1,5},{5,1},{2,6},{6,2},{3,7},{7,3},{8,12},{12,8},{9,1... | collective-permute-start | bytes 3145736 | tf_op jit(solution)/shard_map/ppermute | solution.py:24
  256.9 22.8 %collective-permute-start.16 = (bf16[512,1024]{1,0:T(8,128)(2,1)S(1)}, bf16[512,1024]{1,0:T(8,128)(2,1)S(1)}, u32[]{:S(2)}, u32[]{:S(2)}) collective-permute-start(bf16[512,1024]{1,0:T(8,128)(2,1)S(1)} %add_convert_fusion.3), channel_id=1, source_target_pairs={{0,8},{8,16},{16,24},{24,0},{1,9},{9,17},{17,25},{25,1},{2,10},{10... | collective-permute-start | bytes 3145736 | tf_op jit(solution)/shard_map/ppermute | solution.py:20
  263.1 35.4 %collective-permute-start.5 = (bf16[512,1024]{1,0:T(8,128)(2,1)}, bf16[512,1024]{1,0:T(8,128)(2,1)S(1)}, u32[]{:S(2)}, u32[]{:S(2)}) collective-permute-start(bf16[512,1024]{1,0:T(8,128)(2,1)} %fusion.33), channel_id=1, source_target_pairs={{0,4},{4,0},{1,5},{5,1},{2,6},{6,2},{3,7},{7,3},{8,12},{12,8},{9,1... | collective-permute-start | bytes 3145736 | tf_op jit(solution)/shard_map/ppermute | solution.py:24
  282.8 21.4 %collective-permute-start.17 = (bf16[512,1024]{1,0:T(8,128)(2,1)}, bf16[512,1024]{1,0:T(8,128)(2,1)S(1)}, u32[]{:S(2)}, u32[]{:S(2)}) collective-permute-start(bf16[512,1024]{1,0:T(8,128)(2,1)} %add_convert_fusion.2), channel_id=1, source_target_pairs={{0,8},{8,16},{16,24},{24,0},{1,9},{9,17},{17,25},{25,1},{2,10},{10... | collective-permute-start | bytes 3145736 | tf_op jit(solution)/shard_map/ppermute | solution.py:20
  288.7 38.6 %collective-permute-start = (bf16[512,1024]{1,0:T(8,128)(2,1)}, bf16[512,1024]{1,0:T(8,128)(2,1)S(1)}, u32[]{:S(2)}, u32[]{:S(2)}) collective-permute-start(bf16[512,1024]{1,0:T(8,128)(2,1)} %fusion.30), channel_id=1, source_target_pairs={{0,4},{4,0},{1,5},{5,1},{2,6},{6,2},{3,7},{7,3},{8,12},{12,8},{9,1... | collective-permute-start | bytes 3145736 | tf_op jit(solution)/shard_map/ppermute | solution.py:24
  307.3 20.6 %collective-permute-start.18 = (bf16[512,1024]{1,0:T(8,128)(2,1)}, bf16[512,1024]{1,0:T(8,128)(2,1)}, u32[]{:S(2)}, u32[]{:S(2)}) collective-permute-start(bf16[512,1024]{1,0:T(8,128)(2,1)} %add_convert_fusion.1), channel_id=1, source_target_pairs={{0,8},{8,16},{16,24},{24,0},{1,9},{9,17},{17,25},{25,1},{2,10},{10... | collective-permute-start | bytes 3145736 | tf_op jit(solution)/shard_map/ppermute | solution.py:20
  (21 other events, 302.9 us)

commit v2 on v1

--- a/solution.py
+++ b/solution.py
@@ -1,6 +1,7 @@
 import jax
 import jax.numpy as jnp
 from jax import lax
+from jax.experimental.layout import Layout, with_layout_constraint
 from jax.sharding import PartitionSpec as P
 
 D = 4096
@@ -68,7 +69,7 @@
             ring = shift(ring, "dp", n_dp, 1)
             acts.append(ring)
 
-        quantized, inside, factor = quantize(weight[0], own_scales)
+        quantized, _, _ = quantize(weight[0], own_scales)
         own_grad = lax.dynamic_slice_in_dim(out_grad, dp * own_count, own_count, 1)
 
         def reduced(grad):
@@ -97,19 +98,25 @@
             own_grad, activations, (((0,), (0,)), ((), ())), preferred_element_type=jnp.float32
         )
         own_total = reduced(own_grad)
+        if grads:
+            grads[0], quantized, products = lax.optimization_barrier((grads[0], quantized, products))
         running = None
         for k in range(1, n_dp):
             grad = gather_rows(grads[k - 1], "col", n_col)
             total = reduced(grad)
             if running is not None:
                 total = total + running.astype(jnp.float32)
-            running = shift(total.astype(jnp.bfloat16), "dp", n_dp, 1)
+            leaving, grad = lax.optimization_barrier((total.astype(jnp.bfloat16), grad))
+            running = shift(leaving, "dp", n_dp, 1)
             act = gather_rows(acts[k - 1], "row", n_row)
             products = products + lax.dot_general(
                 grad, act, (((0,), (0,)), ((), ())), preferred_element_type=jnp.float32
             )
         if running is not None:
             own_total = own_total + running.astype(jnp.float32)
+        products, latent = lax.optimization_barrier((products, weight[0]))
+        products = with_layout_constraint(products, Layout((0, 1)))
+        _, inside, factor = quantize(latent, own_scales)
         input_grad = own_total.astype(jnp.bfloat16)
         step_rows = lax.psum(jnp.sum(products * factor, axis=1) * grad_factor, "col")
         weight_grad = (products * inside)[None]

time: 331 us -> 321 us (0.970)
  local copies, waits for them, and re-layouts: 24.9 us -> 5.99 us
  starting transfers between devices: 27.4 us -> 46 us
  matrix products: 64 us -> 59 us
  other arithmetic: 27.8 us -> 24 us
    ppermute x9, waiting for transfers between devices: 115 us -> 82 us  [shift(): lax.ppermute(block, axis, [(i, (i + by) % count) for i in range(count)])]
    ppermute x16, waiting for transfers between devices: 63.8 us -> 95.4 us  [swap(): return lax.ppermute(block, axis, [(i, i ^ bit) for i in range(count)])]
    unnamed x42 -> x20, local copies, waits for them, and re-layouts: 18.4 us -> 0.05 us
    ppermute x9, starting transfers between devices: 15 us -> 33 us  [shift(): lax.ppermute(block, axis, [(i, (i + by) % count) for i in range(count)])]
    concatenate x3, other arithmetic: 7.51 us -> 1.04 us  [gather_rows(): return jnp.concatenate(parts, axis=0)]
    convert_element_type x0 -> x1, other arithmetic: none -> 5.23 us  [quantize(): quantized = (levels * scales[:, None]).astype(jnp.bfloat16)]
  transfers between devices with their start and end apart: 25 -> 25, of which waited for: 14 -> 9; matrix products, arithmetic and copies ran while one was open for 26% -> 25% of each run, Pallas kernels for 0% -> 0%
where the time goes in v2:
time: 321 us; the launch traced here: 320 us
  waiting for transfers between devices  177 us (55%)
  matrix products  59 us (18%)
  starting transfers between devices  46 us (14%)
  other arithmetic  24 us (7%)
  blocking collectives  7.12 us (2%)
  local copies, waits for them, and re-layouts  5.99 us (2%)
    ppermute x16, waiting for transfers between devices, swap(): return lax.ppermute(block, axis, [(i, i ^ bit) for i in range(count)])  95.4 us
    ppermute x9, waiting for transfers between devices, shift(): lax.ppermute(block, axis, [(i, (i + by) % count) for i in range(count)])  82 us
    ppermute x9, starting transfers between devices, shift(): lax.ppermute(block, axis, [(i, (i + by) % count) for i in range(count)])  33 us
    dot_general x3, matrix products, shards(): lax.dot_general(grad, act, (((0,), (0,)), ((), ())), preferred_element_ty...  25.2 us
    dot_general x4, matrix products, reduced(): jnp.dot(kept, quantized, preferred_element_type=jnp.float32)  13.8 us
    ppermute x16, starting transfers between devices, swap(): return lax.ppermute(block, axis, [(i, i ^ bit) for i in range(count)])  13 us
    dot_general x4, matrix products, reduced(): jnp.dot(sent, quantized, preferred_element_type=jnp.float32)  11.9 us
    select_n x6, other arithmetic, gather_rows(): jnp.where(flag, parts[key ^ bit], parts[key])  8.27 us
  transfers between devices with their start and end apart: 25, of which 9 were waited for; matrix products, arithmetic and copies ran while one was open for 25% of the time, Pallas kernels for 0%

profile of v2, /device:TPU:0, one launch (start us, length us, event | category | flops | bytes accessed | tf_op | source)
XLA Modules:
  0.0 320.4 jit_solution(8986064453611099961)
XLA Ops:
  0.7 5.1 %fusion.58 = (bf16[256,1792]{1,0:T(8,128)(2,1)}, bf16[256,1792]{1,0:T(8,128)(2,1)}, bf16[256,1792]{1,0:T(8,128)(2,1)}) fusion(bf16[1024,7168]{1,0:T(8,128)(2,1)} %param.5, s32[]{:T(128)S(6)} %select_n.223, s32[]{:T(128)S(6)} %select_n.226, s32[]{:T(128)S(6)} %select_n.237, s32[]{:T(128)S(6)} %select_n.240), kind=kLoop, calls=%fused_computation.91 | loop fusion | bytes 5505040 | tf_op jit(solution)/shard_map/dynamic_slice | solution.py:67
  5.9 3.0 collective-permute-start.5
  12.4 5.2 %multiply_convert_fusion = bf16[1792,1024]{1,0:T(8,128)(2,1)} fusion(f32[1792]{0:T(1024)S(1)} %dynamic-slice_reduce_fusion, f32[1,1792,1024]{2,1,0:T(8,128)} %param.6), kind=kLoop, calls=%fused_computation.5 | loop fusion | flops 11010048 | bytes 11017216 | tf_op jit(solution)/shard_map/convert_element_type | solution.py:16
  17.6 8.1 %fusion.1 = f32[1792,1024]{1,0:T(8,128)} fusion(bf16[1024,1024]{1,0:T(8,128)(2,1)S(1)} %copy-done, bf16[1024,7168]{1,0:T(8,128)(2,1)} %param.5, s32[]{:T(128)S(6)} %select_n.216), kind=kOutput, calls=%fused_computation.10 | convolution fusion | flops 3758096384 | bytes 13107204 | tf_op jit(solution)/shard_map/dot_general | solution.py:97
  25.7 6.8 %collective-permute-done.5 = bf16[256,1792]{1,0:T(8,128)(2,1)} collective-permute-done((bf16[256,1792]{1,0:T(8,128)(2,1)}, bf16[256,1792]{1,0:T(8,128)(2,1)}, u32[]{:S(2)}, u32[]{:S(2)}) %collective-permute-start.5) | collective-permute-done | bytes 917536 | tf_op jit(solution)/shard_map/ppermute | solution.py:21
  36.6 57.0 %collective-permute-done.7 = bf16[256,1792]{1,0:T(8,128)(2,1)} collective-permute-done((bf16[256,1792]{1,0:T(8,128)(2,1)}, bf16[256,1792]{1,0:T(8,128)(2,1)}, u32[]{:S(2)}, u32[]{:S(2)}) %collective-permute-start.7) | collective-permute-done | bytes 917536 | tf_op jit(solution)/shard_map/ppermute | solution.py:21
  96.5 6.4 %fusion.28 = f32[512,1024]{1,0:T(8,128)} fusion(bf16[1792,1024]{1,0:T(8,128)(2,1)} %multiply_convert_fusion, bf16[1024,7168]{1,0:T(8,128)(2,1)} %param.5, s32[]{:T(128)S(6)} %select_n.215, s32[]{:T(128)S(6)} %select_n.217), kind=kOutput, calls=%fused_computation.42 | convolution fusion | flops 1879048192 | bytes 7602184 | tf_op jit(solution)/shard_map/dot_general | solution.py:86
  103.0 5.7 %fusion.30 = bf16[512,1024]{1,0:T(8,128)(2,1)} fusion(bf16[1792,1024]{1,0:T(8,128)(2,1)} %multiply_convert_fusion, bf16[1024,7168]{1,0:T(8,128)(2,1)} %param.5, s32[]{:T(128)S(6)} %select_n.219, s32[]{:T(128)S(6)} %select_n.217), kind=kOutput, calls=%fused_computation.44 | convolution fusion | flops 1879572480 | bytes 6553608 | tf_op jit(solution)/shard_map/dot_general | solution.py:84
  108.7 11.2 %collective-permute-done.20 = bf16[512,1024]{1,0:T(8,128)(2,1)S(1)} collective-permute-done((bf16[512,1024]{1,0:T(8,128)(2,1)}, bf16[512,1024]{1,0:T(8,128)(2,1)S(1)}, u32[]{:S(2)}, u32[]{:S(2)}) %collective-permute-start.20) | collective-permute-done | bytes 1048608 | tf_op jit(solution)/shard_map/ppermute | solution.py:25
  119.9 16.1 %collective-permute-start.21 = (bf16[512,1024]{1,0:T(8,128)(2,1)}, bf16[512,1024]{1,0:T(8,128)(2,1)S(1)}, u32[]{:S(2)}, u32[]{:S(2)}) collective-permute-start(bf16[512,1024]{1,0:T(8,128)(2,1)} %collective-permute-done.19), channel_id=1, source_target_pairs={{0,8},{8,16},{16,24},{24,0},{1,9},{9,17},{17,25},{25,1},{2,10},{10... | collective-permute-start | bytes 3145736 | tf_op jit(solution)/shard_map/ppermute | solution.py:21
  143.6 18.5 %collective-permute-done.2 = bf16[256,1792]{1,0:T(8,128)(2,1)S(1)} collective-permute-done((bf16[256,1792]{1,0:T(8,128)(2,1)}, bf16[256,1792]{1,0:T(8,128)(2,1)S(1)}, u32[]{:S(2)}, u32[]{:S(2)}) %collective-permute-start.2) | collective-permute-done | bytes 917536 | tf_op jit(solution)/shard_map/ppermute | solution.py:25
  177.4 12.2 %collective-permute-done.23 = bf16[512,1024]{1,0:T(8,128)(2,1)S(1)} collective-permute-done((bf16[512,1024]{1,0:T(8,128)(2,1)S(1)}, bf16[512,1024]{1,0:T(8,128)(2,1)S(1)}, u32[]{:S(2)}, u32[]{:S(2)}) %collective-permute-start.23) | collective-permute-done | bytes 1048608 | tf_op jit(solution)/shard_map/ppermute | solution.py:21
  191.2 19.4 %collective-permute-done.15 = bf16[512,1024]{1,0:T(8,128)(2,1)S(1)} collective-permute-done((bf16[512,1024]{1,0:T(8,128)(2,1)S(1)}, bf16[512,1024]{1,0:T(8,128)(2,1)S(1)}, u32[]{:S(2)}, u32[]{:S(2)}) %collective-permute-start.15) | collective-permute-done | bytes 1048608 | tf_op jit(solution)/shard_map/ppermute | solution.py:25
  213.1 2.6 collective-permute-start.16
  215.9 6.1 %fusion.3 = f32[1792,1024]{1,0:T(8,128)} fusion(bf16[1024,1792]{1,0:T(8,128)(2,1)S(1)} %pad_maximum_fusion.2, bf16[512,1024]{1,0:T(8,128)(2,1)S(1)} %get-tuple-element.45, bf16[512,1024]{1,0:T(8,128)(2,1)S(1)} %get-tuple-element.44), kind=kOutput, calls=%fused_computation.13 | convolution fusion | flops 3762290688 | bytes 13107200 | tf_op jit(solution)/shard_map/dot_general | solution.py:112
  222.0 11.0 %collective-permute-done.11 = bf16[512,1024]{1,0:T(8,128)(2,1)S(1)} collective-permute-done((bf16[512,1024]{1,0:T(8,128)(2,1)S(1)}, bf16[512,1024]{1,0:T(8,128)(2,1)S(1)}, u32[]{:S(2)}, u32[]{:S(2)}) %collective-permute-start.11) | collective-permute-done | bytes 1048608 | tf_op jit(solution)/shard_map/ppermute | solution.py:25
  233.0 6.0 %collective-permute-done.16 = bf16[512,1024]{1,0:T(8,128)(2,1)S(1)} collective-permute-done((bf16[512,1024]{1,0:T(8,128)(2,1)S(1)}, bf16[512,1024]{1,0:T(8,128)(2,1)S(1)}, u32[]{:S(2)}, u32[]{:S(2)}) %collective-permute-start.16) | collective-permute-done | bytes 1048608 | tf_op jit(solution)/shard_map/ppermute | solution.py:21
  242.2 35.3 %collective-permute-done.24 = bf16[512,1024]{1,0:T(8,128)(2,1)S(1)} collective-permute-done((bf16[512,1024]{1,0:T(8,128)(2,1)S(1)}, bf16[512,1024]{1,0:T(8,128)(2,1)S(1)}, u32[]{:S(2)}, u32[]{:S(2)}) %collective-permute-start.24) | collective-permute-done | bytes 1048608 | tf_op jit(solution)/shard_map/ppermute | solution.py:25
  279.0 6.1 %fusion.7 = f32[1792,1024]{1,0:T(8,128)} fusion(bf16[1024,1792]{1,0:T(8,128)(2,1)S(1)} %pad_maximum_fusion.1, bf16[512,1024]{1,0:T(8,128)(2,1)S(1)} %get-tuple-element.47, bf16[512,1024]{1,0:T(8,128)(2,1)S(1)} %get-tuple-element.46), kind=kOutput, calls=%fused_computation.17 | convolution fusion | flops 3762290688 | bytes 13107200 | tf_op jit(solution)/shard_map/dot_general | solution.py:112
  285.1 3.1 add_convert_fusion.1
  290.8 13.0 %add_add_fusion = f32[1792,1024]{1,0:T(8,128)S(1)} fusion(f32[1792,1024]{1,0:T(8,128)} %fusion.7, f32[1792,1024]{1,0:T(8,128)} %fusion.1, f32[1792,1024]{1,0:T(8,128)} %fusion.3, bf16[1024,1792]{1,0:T(8,128)(2,1)} %copy-done.2, bf16[512,1024]{1,0:T(8,128)(2,1)S(1)} %copy-done.5, bf16[512,1024]{1,0:T(8,128)(2,1)S(1)} %copy-done.4), kind=kOutput, calls=%fused_computation.4 | convolution fusion | flops 3767795712 | bytes 35127296 | tf_op jit(solution)/shard_map/dot_general | solution.py:112
  303.9 6.0 %multiply_reduce_fusion = (f32[1792]{0:T(1024)S(1)}, f32[1,1792,1024]{2,1,0:T(8,128)}) fusion(f32[1792,1024]{1,0:T(8,128)S(1)} %add_add_fusion, f32[1792,1024]{1,0:T(8,128)S(1)} %bitcast.18, f32[1792]{0:T(1024)S(1)} %dynamic-slice_reduce_fusion), kind=kLoop, calls=%fused_computation.3 | loop fusion | flops 25688320 | bytes 22034432 | tf_op jit(solution)/shard_map/reduce_sum | solution.py:121
  309.9 7.1 %psum.7 = f32[1,1792]{1,0:T(1,128)} all-reduce(f32[1,1792]{1,0:T(1,128)S(1)} %broadcast_in_dim.20), channel_id=1, replica_groups=mesh['dp'=4,'row'=2,'col'=4] {'col'}, use_global_device_ids=true, to_apply=%region_1.2 | all-reduce | flops 1792 | bytes 14336 | tf_op jit(solution)/shard_map/psum | solution.py:121
  317.0 3.4 %add_convert_fusion = bf16[512,1024]{1,0:T(8,128)(2,1)} fusion(bf16[512,1024]{1,0:T(8,128)(2,1)} %collective-permute-done.18, f32[512,1024]{1,0:T(8,128)} %fusion.28, bf16[512,1024]{1,0:T(8,128)(2,1)S(1)} %collective-permute-done), kind=kLoop, calls=%fused_computation.24 | loop fusion | flops 2621440 | bytes 5242880 | tf_op jit(solution)/shard_map/convert_element_type | solution.py:120
  (77 shorter events, 44.8 us)
Async XLA Ops:
  5.9 26.7 %collective-permute-start.5 = (bf16[256,1792]{1,0:T(8,128)(2,1)}, bf16[256,1792]{1,0:T(8,128)(2,1)}, u32[]{:S(2)}, u32[]{:S(2)}) collective-permute-start(bf16[256,1792]{1,0:T(8,128)(2,1)} %get-tuple-element.28), channel_id=1, source_target_pairs={{0,8},{8,16},{16,24},{24,0},{1,9},{9,17},{17,25},{25,1},{2,10},{10... | collective-permute-start | bytes 2752520 | tf_op jit(solution)/shard_map/ppermute | solution.py:21
  8.9 84.6 %collective-permute-start.7 = (bf16[256,1792]{1,0:T(8,128)(2,1)}, bf16[256,1792]{1,0:T(8,128)(2,1)}, u32[]{:S(2)}, u32[]{:S(2)}) collective-permute-start(bf16[256,1792]{1,0:T(8,128)(2,1)} %get-tuple-element.29), channel_id=1, source_target_pairs={{0,16},{8,24},{16,0},{24,8},{1,17},{9,25},{17,1},{25,9},{2,18},{10... | collective-permute-start | bytes 2752520 | tf_op jit(solution)/shard_map/ppermute | solution.py:21
  11.6 83.4 %collective-permute-start.19 = (bf16[512,1024]{1,0:T(8,128)(2,1)S(1)}, bf16[512,1024]{1,0:T(8,128)(2,1)}, u32[]{:S(2)}, u32[]{:S(2)}) collective-permute-start(bf16[512,1024]{1,0:T(8,128)(2,1)S(1)} %constant_dynamic-slice_fusion), channel_id=1, source_target_pairs={{0,8},{8,16},{16,24},{24,0},{1,9},{9,17},{17,25},{25,1},{2,10},{10... | collective-permute-start | bytes 3145736 | tf_op jit(solution)/shard_map/ppermute | solution.py:21
  32.6 64.0 %collective-permute-start.12 = (bf16[256,1792]{1,0:T(8,128)(2,1)}, bf16[256,1792]{1,0:T(8,128)(2,1)S(1)}, u32[]{:S(2)}, u32[]{:S(2)}) collective-permute-start(bf16[256,1792]{1,0:T(8,128)(2,1)} %collective-permute-done.5), channel_id=1, source_target_pairs={{0,2},{1,3},{2,0},{3,1},{4,6},{5,7},{6,4},{7,5},{8,10},{9,11},{10,... | collective-permute-start | bytes 2752520 | tf_op jit(solution)/shard_map/ppermute | solution.py:25
  34.3 103.2 %collective-permute-start.1 = (bf16[256,1792]{1,0:T(8,128)(2,1)}, bf16[256,1792]{1,0:T(8,128)(2,1)}, u32[]{:S(2)}, u32[]{:S(2)}) collective-permute-start(bf16[256,1792]{1,0:T(8,128)(2,1)} %get-tuple-element.27), channel_id=1, source_target_pairs={{0,24},{8,0},{16,8},{24,16},{1,25},{9,1},{17,9},{25,17},{2,26},{10... | collective-permute-start | bytes 2752520 | tf_op jit(solution)/shard_map/ppermute | solution.py:21
  36.6 102.5 %collective-permute-start.14 = (bf16[256,1792]{1,0:T(8,128)(2,1)}, bf16[256,1792]{1,0:T(8,128)(2,1)}, u32[]{:S(2)}, u32[]{:S(2)}) collective-permute-start(bf16[256,1792]{1,0:T(8,128)(2,1)} %collective-permute-done.5), channel_id=1, source_target_pairs={{0,1},{1,0},{2,3},{3,2},{4,5},{5,4},{6,7},{7,6},{8,9},{9,8},{10,11... | collective-permute-start | bytes 2752520 | tf_op jit(solution)/shard_map/ppermute | solution.py:25
  93.5 45.5 %collective-permute-start.8 = (bf16[256,1792]{1,0:T(8,128)(2,1)}, bf16[256,1792]{1,0:T(8,128)(2,1)}, u32[]{:S(2)}, u32[]{:S(2)}) collective-permute-start(bf16[256,1792]{1,0:T(8,128)(2,1)} %collective-permute-done.7), channel_id=1, source_target_pairs={{0,2},{1,3},{2,0},{3,1},{4,6},{5,7},{6,4},{7,5},{8,10},{9,11},{10,... | collective-permute-start | bytes 2752520 | tf_op jit(solution)/shard_map/ppermute | solution.py:25
  95.0 24.9 %collective-permute-start.20 = (bf16[512,1024]{1,0:T(8,128)(2,1)}, bf16[512,1024]{1,0:T(8,128)(2,1)S(1)}, u32[]{:S(2)}, u32[]{:S(2)}) collective-permute-start(bf16[512,1024]{1,0:T(8,128)(2,1)} %collective-permute-done.19), channel_id=1, source_target_pairs={{0,4},{4,0},{1,5},{5,1},{2,6},{6,2},{3,7},{7,3},{8,12},{12,8},{9,1... | collective-permute-start | bytes 3145736 | tf_op jit(solution)/shard_map/ppermute | solution.py:25
  96.5 44.0 %collective-permute-start.13 = (bf16[256,1792]{1,0:T(8,128)(2,1)S(1)}, bf16[256,1792]{1,0:T(8,128)(2,1)}, u32[]{:S(2)}, u32[]{:S(2)}) collective-permute-start(bf16[256,1792]{1,0:T(8,128)(2,1)S(1)} %collective-permute-done.12), channel_id=1, source_target_pairs={{0,1},{1,0},{2,3},{3,2},{4,5},{5,4},{6,7},{7,6},{8,9},{9,8},{10,11... | collective-permute-start | bytes 2752520 | tf_op jit(solution)/shard_map/ppermute | solution.py:25
  119.9 42.1 %collective-permute-start.21 = (bf16[512,1024]{1,0:T(8,128)(2,1)}, bf16[512,1024]{1,0:T(8,128)(2,1)S(1)}, u32[]{:S(2)}, u32[]{:S(2)}) collective-permute-start(bf16[512,1024]{1,0:T(8,128)(2,1)} %collective-permute-done.19), channel_id=1, source_target_pairs={{0,8},{8,16},{16,24},{24,0},{1,9},{9,17},{17,25},{25,1},{2,10},{10... | collective-permute-start | bytes 3145736 | tf_op jit(solution)/shard_map/ppermute | solution.py:21
  137.5 179.5 %collective-permute-start = (bf16[512,1024]{1,0:T(8,128)(2,1)}, bf16[512,1024]{1,0:T(8,128)(2,1)S(1)}, u32[]{:S(2)}, u32[]{:S(2)}) collective-permute-start(bf16[512,1024]{1,0:T(8,128)(2,1)} %fusion.30), channel_id=1, source_target_pairs={{0,4},{4,0},{1,5},{5,1},{2,6},{6,2},{3,7},{7,3},{8,12},{12,8},{9,1... | collective-permute-start | bytes 3145736 | tf_op jit(solution)/shard_map/ppermute | solution.py:25
  139.1 23.0 %collective-permute-start.2 = (bf16[256,1792]{1,0:T(8,128)(2,1)}, bf16[256,1792]{1,0:T(8,128)(2,1)S(1)}, u32[]{:S(2)}, u32[]{:S(2)}) collective-permute-start(bf16[256,1792]{1,0:T(8,128)(2,1)} %collective-permute-done.1), channel_id=1, source_target_pairs={{0,2},{1,3},{2,0},{3,1},{4,6},{5,7},{6,4},{7,5},{8,10},{9,11},{10,... | collective-permute-start | bytes 2752520 | tf_op jit(solution)/shard_map/ppermute | solution.py:25
  140.6 22.0 %collective-permute-start.9 = (bf16[256,1792]{1,0:T(8,128)(2,1)}, bf16[256,1792]{1,0:T(8,128)(2,1)S(1)}, u32[]{:S(2)}, u32[]{:S(2)}) collective-permute-start(bf16[256,1792]{1,0:T(8,128)(2,1)} %collective-permute-done.8), channel_id=1, source_target_pairs={{0,1},{1,0},{2,3},{3,2},{4,5},{5,4},{6,7},{7,6},{8,9},{9,8},{10,11... | collective-permute-start | bytes 2752520 | tf_op jit(solution)/shard_map/ppermute | solution.py:25
  143.1 28.3 %collective-permute-start.4 = (bf16[256,1792]{1,0:T(8,128)(2,1)}, bf16[256,1792]{1,0:T(8,128)(2,1)S(1)}, u32[]{:S(2)}, u32[]{:S(2)}) collective-permute-start(bf16[256,1792]{1,0:T(8,128)(2,1)} %collective-permute-done.1), channel_id=1, source_target_pairs={{0,1},{1,0},{2,3},{3,2},{4,5},{5,4},{6,7},{7,6},{8,9},{9,8},{10,11... | collective-permute-start | bytes 2752520 | tf_op jit(solution)/shard_map/ppermute | solution.py:25
  162.0 11.0 %collective-permute-start.3 = (bf16[256,1792]{1,0:T(8,128)(2,1)S(1)}, bf16[256,1792]{1,0:T(8,128)(2,1)S(1)}, u32[]{:S(2)}, u32[]{:S(2)}) collective-permute-start(bf16[256,1792]{1,0:T(8,128)(2,1)S(1)} %collective-permute-done.2), channel_id=1, source_target_pairs={{0,1},{1,0},{2,3},{3,2},{4,5},{5,4},{6,7},{7,6},{8,9},{9,8},{10,11... | collective-permute-start | bytes 2752520 | tf_op jit(solution)/shard_map/ppermute | solution.py:25
  162.0 51.1 %collective-permute-start.22 = (bf16[512,1024]{1,0:T(8,128)(2,1)S(1)}, bf16[512,1024]{1,0:T(8,128)(2,1)S(1)}, u32[]{:S(2)}, u32[]{:S(2)}) collective-permute-start(bf16[512,1024]{1,0:T(8,128)(2,1)S(1)} %collective-permute-done.21), channel_id=1, source_target_pairs={{0,4},{4,0},{1,5},{5,1},{2,6},{6,2},{3,7},{7,3},{8,12},{12,8},{9,1... | collective-permute-start | bytes 3145736 | tf_op jit(solution)/shard_map/ppermute | solution.py:25
  162.6 27.1 %collective-permute-start.23 = (bf16[512,1024]{1,0:T(8,128)(2,1)S(1)}, bf16[512,1024]{1,0:T(8,128)(2,1)S(1)}, u32[]{:S(2)}, u32[]{:S(2)}) collective-permute-start(bf16[512,1024]{1,0:T(8,128)(2,1)S(1)} %collective-permute-done.21), channel_id=1, source_target_pairs={{0,8},{8,16},{16,24},{24,0},{1,9},{9,17},{17,25},{25,1},{2,10},{10... | collective-permute-start | bytes 3145736 | tf_op jit(solution)/shard_map/ppermute | solution.py:21
  171.4 39.1 %collective-permute-start.15 = (bf16[512,1024]{1,0:T(8,128)(2,1)S(1)}, bf16[512,1024]{1,0:T(8,128)(2,1)S(1)}, u32[]{:S(2)}, u32[]{:S(2)}) collective-permute-start(bf16[512,1024]{1,0:T(8,128)(2,1)S(1)} %fusion.39), channel_id=1, source_target_pairs={{0,4},{4,0},{1,5},{5,1},{2,6},{6,2},{3,7},{7,3},{8,12},{12,8},{9,1... | collective-permute-start | bytes 3145736 | tf_op jit(solution)/shard_map/ppermute | solution.py:25
  173.0 60.0 %collective-permute-start.11 = (bf16[512,1024]{1,0:T(8,128)(2,1)S(1)}, bf16[512,1024]{1,0:T(8,128)(2,1)S(1)}, u32[]{:S(2)}, u32[]{:S(2)}) collective-permute-start(bf16[512,1024]{1,0:T(8,128)(2,1)S(1)} %fusion.36), channel_id=1, source_target_pairs={{0,4},{4,0},{1,5},{5,1},{2,6},{6,2},{3,7},{7,3},{8,12},{12,8},{9,1... | collective-permute-start | bytes 3145736 | tf_op jit(solution)/shard_map/ppermute | solution.py:25
  189.7 95.4 %collective-permute-start.6 = (bf16[512,1024]{1,0:T(8,128)(2,1)S(1)}, bf16[512,1024]{1,0:T(8,128)(2,1)S(1)}, u32[]{:S(2)}, u32[]{:S(2)}) collective-permute-start(bf16[512,1024]{1,0:T(8,128)(2,1)S(1)} %fusion.33), channel_id=1, source_target_pairs={{0,4},{4,0},{1,5},{5,1},{2,6},{6,2},{3,7},{7,3},{8,12},{12,8},{9,1... | collective-permute-start | bytes 3145736 | tf_op jit(solution)/shard_map/ppermute | solution.py:25
  210.5 67.0 %collective-permute-start.24 = (bf16[512,1024]{1,0:T(8,128)(2,1)S(1)}, bf16[512,1024]{1,0:T(8,128)(2,1)S(1)}, u32[]{:S(2)}, u32[]{:S(2)}) collective-permute-start(bf16[512,1024]{1,0:T(8,128)(2,1)S(1)} %collective-permute-done.23), channel_id=1, source_target_pairs={{0,4},{4,0},{1,5},{5,1},{2,6},{6,2},{3,7},{7,3},{8,12},{12,8},{9,1... | collective-permute-start | bytes 3145736 | tf_op jit(solution)/shard_map/ppermute | solution.py:25
  213.1 25.8 %collective-permute-start.16 = (bf16[512,1024]{1,0:T(8,128)(2,1)S(1)}, bf16[512,1024]{1,0:T(8,128)(2,1)S(1)}, u32[]{:S(2)}, u32[]{:S(2)}) collective-permute-start(bf16[512,1024]{1,0:T(8,128)(2,1)S(1)} %add_convert_fusion.3), channel_id=1, source_target_pairs={{0,8},{8,16},{16,24},{24,0},{1,9},{9,17},{17,25},{25,1},{2,10},{10... | collective-permute-start | bytes 3145736 | tf_op jit(solution)/shard_map/ppermute | solution.py:21
  241.1 43.9 %collective-permute-start.17 = (bf16[512,1024]{1,0:T(8,128)(2,1)S(1)}, bf16[512,1024]{1,0:T(8,128)(2,1)S(1)}, u32[]{:S(2)}, u32[]{:S(2)}) collective-permute-start(bf16[512,1024]{1,0:T(8,128)(2,1)S(1)} %add_convert_fusion.2), channel_id=1, source_target_pairs={{0,8},{8,16},{16,24},{24,0},{1,9},{9,17},{17,25},{25,1},{2,10},{10... | collective-permute-start | bytes 3145736 | tf_op jit(solution)/shard_map/ppermute | solution.py:21
  288.2 28.8 %collective-permute-start.18 = (bf16[512,1024]{1,0:T(8,128)(2,1)}, bf16[512,1024]{1,0:T(8,128)(2,1)}, u32[]{:S(2)}, u32[]{:S(2)}) collective-permute-start(bf16[512,1024]{1,0:T(8,128)(2,1)} %add_convert_fusion.1), channel_id=1, source_target_pairs={{0,8},{8,16},{16,24},{24,0},{1,9},{9,17},{17,25},{25,1},{2,10},{10... | collective-permute-start | bytes 3145736 | tf_op jit(solution)/shard_map/ppermute | solution.py:21
  (11 other events, 246.8 us)
